TPU v7x, 32 devices: a whole 2x2x4 slice. The times are simulated.
32 devices in a mesh: rep: 4 (over x, core), shard: 8 (over z, y).
Axes of the slice: x: 2, y: 2, z: 4, core: 2. Of those that a mesh axis runs over, the one named last changes fastest.
Arguments:
- grads: float32 [4, 8, 16, 128, 128], P('rep', 'shard'), may hold values from -24 to 24
- counts: int32 [4, 8, 16, 128], P('rep', 'shard'), may hold values from 0 to 5
- block_owner: int32 [4, 8, 16, 1], P('rep', 'shard'), may hold values from 0 to 7; in each aligned block of 16 rows (0 to 15, 16 to 31, ..., all dimensions but the last counted through in order) at most 4 rows name the same one
- block_local: int32 [4, 8, 16], P('rep', 'shard'), may hold values from 0 to 63
Outputs:
- clipped: float32 [512, 128, 128], P('shard', 'rep')
Inputs may be any that keep to these rules, and one draw needn't show every extreme that they name: `block_owner`: among the 16 blocks of one device no owner is named more than 4 times, a bound that some block reaches.
All inputs are finite; a program needn't handle non-finite values.
Results may differ from a plain program's by a relative error of at most 0.0003.
Values sent between devices are 32-bit elements; how exact they have to be, the bound alone decides.
A program may use at most 128 MiB of HBM per device.

v0:
```python
import math

import jax
import jax.numpy as jnp
from jax import lax
from jax.sharding import PartitionSpec as P

BLK_SHARD = 64
CAP = 4


def accumulate(values, tallies, indices, owned):
    slots = indices.shape[0]
    onehot = (jnp.arange(owned, dtype=jnp.int32)[:, None] == indices[None, :]).astype(jnp.float32)
    sums = jnp.dot(
        onehot,
        values.reshape(slots, -1),
        precision=lax.Precision.HIGHEST,
        preferred_element_type=jnp.float32,
    )
    totals = jnp.dot(
        onehot, tallies, precision=lax.Precision.HIGHEST, preferred_element_type=jnp.float32
    )
    return (sums.reshape(owned, values.shape[1], values.shape[2]), totals)


def local(grads, counts, block_owner, block_local):
    nshard = lax.axis_size("shard")
    nrep = lax.axis_size("rep")
    nblocks = grads.shape[2]
    rows = grads.shape[3]
    width = grads.shape[4]
    owners = block_owner.reshape(nblocks)
    local_ids = block_local.reshape(nblocks)
    blocks = grads.reshape(nblocks, rows, width)
    tallies = counts.reshape(nblocks, rows)
    masked = jnp.where(tallies[..., None] > 0, blocks, jnp.float32(0.0))
    owner_hot = (owners[:, None] == jnp.arange(nshard, dtype=jnp.int32)[None, :]).astype(jnp.int32)
    ranking = jnp.sum(jnp.cumsum(owner_hot, axis=0) * owner_hot, axis=1) - 1
    slot_of = owners * CAP + ranking
    send_vals = jnp.zeros((nshard * CAP, rows, width), jnp.float32).at[slot_of].set(masked)
    send_vals = send_vals.reshape(nshard, CAP, rows, width)
    send_cnts = (
        jnp.zeros((nshard * CAP, rows), jnp.float32).at[slot_of].set(tallies.astype(jnp.float32))
    )
    send_cnts = send_cnts.reshape(nshard, CAP, rows)
    send_ids = (
        jnp.full((nshard * CAP,), -1, jnp.int32).at[slot_of].set(local_ids).reshape(nshard, CAP)
    )
    part_rows = rows // nrep
    id_parts = jnp.broadcast_to(send_ids[:, :, None], (nshard, CAP, nrep))
    got_vals, got_cnts, got_ids = (
        lax.all_to_all(
            lax.all_to_all(send_vals, "rep", split_axis=2, concat_axis=1, tiled=True),
            "shard",
            split_axis=0,
            concat_axis=0,
            tiled=True,
        ),
        lax.all_to_all(
            lax.all_to_all(send_cnts, "rep", split_axis=2, concat_axis=1, tiled=True),
            "shard",
            split_axis=0,
            concat_axis=0,
            tiled=True,
        ),
        lax.all_to_all(
            lax.all_to_all(id_parts, "rep", split_axis=2, concat_axis=1, tiled=True),
            "shard",
            split_axis=0,
            concat_axis=0,
            tiled=True,
        ),
    )
    sums, totals = accumulate(
        got_vals.reshape(-1, part_rows, width),
        got_cnts.reshape(-1, part_rows),
        got_ids.reshape(-1),
        BLK_SHARD,
    )
    mean = sums / jnp.maximum(totals, jnp.float32(1.0))[..., None]
    norm2 = lax.psum(jnp.sum(mean * mean), ("rep", "shard"))
    limit = jnp.float32(0.2 * math.sqrt(BLK_SHARD * nshard * rows * width))
    scale = jnp.minimum(jnp.float32(1.0), limit / jnp.sqrt(norm2 + jnp.float32(1e-06)))
    return mean * scale


def solution(mesh):
    return jax.shard_map(
        local,
        mesh=mesh,
        in_specs=(
            P("rep", "shard", None, None, None),
            P("rep", "shard", None, None),
            P("rep", "shard", None, None),
            P("rep", "shard", None),
        ),
        out_specs=P("shard", "rep", None),
        check_vma=False,
    )
```

profile of v0, /device:TPU:0, one launch (start us, length us, event | category | flops | bytes accessed | tf_op | source)
XLA Modules:
  0.0 169.1 jit_solution(11592075151269960630)
XLA Ops:
  0.0 0.7 fusion.8
  0.8 0.8 select_reduce_fusion
  1.6 0.7 fusion.9
  2.3 0.8 scatter_custom_fusion
  3.0 0.1 broadcast_in_dim.35
  3.1 0.1 copy.57
  3.2 7.8 %all_to_all.69 = s32[8,4,4]{0,1,2:T(4,128)S(1)} all-to-all(s32[8,4,4]{0,1,2:T(4,128)S(1)} %broadcast_in_dim.36), channel_id=1, replica_groups=mesh['rep'=4,'shard'=8] {'rep'}, dimensions={2} | all-to-all | bytes 1024 | tf_op jit(solution)/shard_map/all_to_all | solution.py:68
  11.0 0.7 copy.60
  11.7 5.8 %all-to-all-start.1 = ((s32[8,16,1]{1,2,0:T(1,128)}), s32[8,16,1]{1,2,0:T(1,128)S(1)}, u32[]{:S(2)}, u32[]{:S(2)}) async-start(s32[8,16,1]{1,2,0:T(1,128)} %copy.60), calls=%async_computation.1 | async-start | bytes 8192 | tf_op jit(solution)/shard_map/all_to_all | solution.py:67
  17.5 0.7 compare_bitcast_fusion
  18.2 0.8 scatter_custom_fusion.2
  19.0 0.2 copy.65
  19.2 0.9 reshape.109
  20.1 4.0 %all-to-all-done.1 = s32[8,16,1]{1,2,0:T(1,128)S(1)} async-done(((s32[8,16,1]{1,2,0:T(1,128)}), s32[8,16,1]{1,2,0:T(1,128)S(1)}, u32[]{:S(2)}, u32[]{:S(2)}) %all-to-all-start.1) | async-done | bytes 544 | tf_op jit(solution)/shard_map/all_to_all | solution.py:67
  24.0 3.3 %all-to-all-start.4 = ((f32[4,1,1024]{2,1,0:T(1,128)}), f32[4,1,1024]{2,1,0:T(1,128)S(1)}, u32[]{:S(2)}, u32[]{:S(2)}) async-start(f32[4,1,1024]{2,1,0:T(1,128)} %reshape.109), calls=%async_computation.4 | async-start | bytes 32768 | tf_op jit(solution)/shard_map/all_to_all | solution.py:61
  27.3 1.6 bitcast_select_fusion
  28.9 0.2 broadcast_in_dim.37
  29.1 1.1 scatter_fusion
  30.2 2.7 %copy.61 = f32[8,4,128,128]{3,1,0,2:T(4,128)} copy(f32[8,4,128,128]{3,2,1,0:T(8,128)S(1)} %bitcast.57) | data formatting | bytes 4194304 | tf_op jit(solution)/shard_map/reshape | solution.py:42
  33.0 0.0 all-to-all-done.4
  33.0 3.6 %all-to-all-start.2 = ((f32[8,4,128,128]{3,1,0,2:T(4,128)}), f32[8,4,128,128]{3,1,0,2:T(4,128)S(1)}, u32[]{:S(2)}, u32[]{:S(2)}) async-start(f32[8,4,128,128]{3,1,0,2:T(4,128)} %copy.61), calls=%async_computation.2 | async-start | bytes 4194304 | tf_op jit(solution)/shard_map/all_to_all | solution.py:54
  36.6 0.5 broadcast.70
  37.1 0.7 reduce.4
  37.8 0.3 reshape.110
  38.1 0.1 copy.67
  38.3 0.7 reshape.111
  39.0 23.2 %all-to-all-done.2 = f32[8,4,128,128]{3,1,0,2:T(4,128)S(1)} async-done(((f32[8,4,128,128]{3,1,0,2:T(4,128)}), f32[8,4,128,128]{3,1,0,2:T(4,128)S(1)}, u32[]{:S(2)}, u32[]{:S(2)}) %all-to-all-start.2) | async-done | bytes 2097184 | tf_op jit(solution)/shard_map/all_to_all | solution.py:54
  62.2 3.3 %all-to-all-start.5 = ((f32[8,1,512]{2,1,0:T(1,128)}), f32[8,1,512]{2,1,0:T(1,128)S(1)}, u32[]{:S(2)}, u32[]{:S(2)}) async-start(f32[8,1,512]{2,1,0:T(1,128)} %reshape.111), calls=%async_computation.5 | async-start | bytes 32768 | tf_op jit(solution)/shard_map/all_to_all | solution.py:60
  65.5 1.2 copy.62
  66.8 1.6 copy.63
  68.3 3.7 %all-to-all-done.5 = f32[8,1,512]{2,1,0:T(1,128)S(1)} async-done(((f32[8,1,512]{2,1,0:T(1,128)}), f32[8,1,512]{2,1,0:T(1,128)S(1)}, u32[]{:S(2)}, u32[]{:S(2)}) %all-to-all-start.5) | async-done | bytes 16416 | tf_op jit(solution)/shard_map/all_to_all | solution.py:60
  72.1 3.6 %all-to-all-start.3 = ((f32[8,16,32,128]{3,2,1,0:T(8,128)}), f32[8,16,32,128]{3,2,1,0:T(8,128)S(1)}, u32[]{:S(2)}, u32[]{:S(2)}) async-start(f32[8,16,32,128]{3,2,1,0:T(8,128)} %bitcast.14), calls=%async_computation.3 | async-start | bytes 4194304 | tf_op jit(solution)/shard_map/all_to_all | solution.py:53
  75.7 0.5 broadcast.69
  76.2 0.7 reduce.3
  76.9 0.1 eq.35
  76.9 0.7 reduce.5
  77.6 0.1 reshape.112
  77.7 0.2 convolution_maximum_fusion
  77.9 44.8 %all-to-all-done.3 = f32[8,16,32,128]{3,2,1,0:T(8,128)S(1)} async-done(((f32[8,16,32,128]{3,2,1,0:T(8,128)}), f32[8,16,32,128]{3,2,1,0:T(8,128)S(1)}, u32[]{:S(2)}, u32[]{:S(2)}) %all-to-all-start.3) | async-done | bytes 2097184 | tf_op jit(solution)/shard_map/all_to_all | solution.py:53
  122.7 3.0 %copy.75 = f32[16,8,32,128]{3,1,2,0:T(8,128)} copy(f32[16,8,32,128]{3,2,1,0:T(8,128)S(1)} %bitcast.58) | data formatting | bytes 4194304
  125.6 1.9 %copy.64 = f32[4096,128]{1,0:T(8,128)S(1)} copy(f32[4096,128]{0,1:T(8,128)} %bitcast.60) | data formatting | bytes 4194304 | tf_op jit(solution)/shard_map/dot_general | solution.py:15
  127.6 2.0 %multiply_reduce_fusion = (f32[]{:T(128)}, f32[64,32,128]{2,0,1:T(8,128)S(1)}) fusion(f32[64,32]{0,1:T(8,128)S(1)} %convolution_maximum_fusion, f32[32,128,128]{2,1,0:T(8,128)S(1)} %bitcast.61, s32[128]{0:T(128)S(1)} %eq.35), kind=kOutput, calls=%fused_computation.7 | convolution fusion | flops 403447808 | bytes 3154436 | tf_op jit(solution)/shard_map/dot_general | solution.py:15
  129.6 37.2 %psum.7 = f32[]{:T(128)} all-reduce(f32[]{:T(128)} %get-tuple-element.5), channel_id=1, replica_groups=mesh['rep'=4,'shard'=8] {'rep','shard'}, use_global_device_ids=true, to_apply=%region_6.7 | all-reduce | flops 1 | bytes 8 | tf_op jit(solution)/shard_map/psum | solution.py:82
  167.5 0.1 broadcast_multiply_fusion
  167.6 1.6 copy.69
  (5 shorter events, 0.1 us)
Async XLA Ops:
  11.7 12.3 %all-to-all-start.1 = ((s32[8,16,1]{1,2,0:T(1,128)}), s32[8,16,1]{1,2,0:T(1,128)S(1)}, u32[]{:S(2)}, u32[]{:S(2)}) async-start(s32[8,16,1]{1,2,0:T(1,128)} %copy.60), calls=%async_computation.1 | async-start | bytes 8192 | tf_op jit(solution)/shard_map/all_to_all | solution.py:67
  24.0 8.9 %all-to-all-start.4 = ((f32[4,1,1024]{2,1,0:T(1,128)}), f32[4,1,1024]{2,1,0:T(1,128)S(1)}, u32[]{:S(2)}, u32[]{:S(2)}) async-start(f32[4,1,1024]{2,1,0:T(1,128)} %reshape.109), calls=%async_computation.4 | async-start | bytes 32768 | tf_op jit(solution)/shard_map/all_to_all | solution.py:61
  33.0 29.2 %all-to-all-start.2 = ((f32[8,4,128,128]{3,1,0,2:T(4,128)}), f32[8,4,128,128]{3,1,0,2:T(4,128)S(1)}, u32[]{:S(2)}, u32[]{:S(2)}) async-start(f32[8,4,128,128]{3,1,0,2:T(4,128)} %copy.61), calls=%async_computation.2 | async-start | bytes 4194304 | tf_op jit(solution)/shard_map/all_to_all | solution.py:54
  62.2 9.9 %all-to-all-start.5 = ((f32[8,1,512]{2,1,0:T(1,128)}), f32[8,1,512]{2,1,0:T(1,128)S(1)}, u32[]{:S(2)}, u32[]{:S(2)}) async-start(f32[8,1,512]{2,1,0:T(1,128)} %reshape.111), calls=%async_computation.5 | async-start | bytes 32768 | tf_op jit(solution)/shard_map/all_to_all | solution.py:60
  72.1 50.6 %all-to-all-start.3 = ((f32[8,16,32,128]{3,2,1,0:T(8,128)}), f32[8,16,32,128]{3,2,1,0:T(8,128)S(1)}, u32[]{:S(2)}, u32[]{:S(2)}) async-start(f32[8,16,32,128]{3,2,1,0:T(8,128)} %bitcast.14), calls=%async_computation.3 | async-start | bytes 4194304 | tf_op jit(solution)/shard_map/all_to_all | solution.py:53
where the time goes:
time: 171 us; the launch traced here: 169 us
  waiting for transfers between devices  75.7 us (44%)
  blocking collectives  45.1 us (26%)
  starting transfers between devices  19.6 us (11%)
  local copies, waits for them, and re-layouts  18.3 us (11%)
  other arithmetic  7.37 us (4%)
  matrix products  2.21 us (1%)
    all_to_all x1, waiting for transfers between devices, local(): lax.all_to_all(lax.all_to_all(send_vals, 'rep', split_axis=2, concat_axis...  44.8 us
    psum x1, blocking collectives, local(): norm2 = lax.psum(jnp.sum(mean * mean), ('rep', 'shard'))  37.2 us
    all_to_all x1, waiting for transfers between devices, local(): lax.all_to_all(send_vals, 'rep', split_axis=2, concat_axis=1, tiled=True)  23.2 us
    all_to_all x1, blocking collectives, local(): lax.all_to_all(id_parts, 'rep', split_axis=2, concat_axis=1, tiled=True)  7.84 us
    all_to_all x1, starting transfers between devices, local(): lax.all_to_all(lax.all_to_all(id_parts, 'rep', split_axis=2, concat_axis=...  5.83 us
    unnamed x5, local copies, waits for them, and re-layouts  4.97 us
    all_to_all x1, waiting for transfers between devices, local(): lax.all_to_all(lax.all_to_all(id_parts, 'rep', split_axis=2, concat_axis=...  3.97 us
    all_to_all x1, waiting for transfers between devices, local(): lax.all_to_all(lax.all_to_all(send_cnts, 'rep', split_axis=2, concat_axis...  3.72 us
  transfers between devices with their start and end apart: 5, of which 4 were waited for; matrix products, arithmetic and copies ran while one was open for 9% of the time, Pallas kernels for 0%

commit v1 on v0

v1 whole, which is shorter than its diff:
```python
import functools
import math

import jax
import jax.numpy as jnp
from jax import lax
from jax.experimental import pallas as pl
from jax.experimental.pallas import tpu as pltpu
from jax.sharding import PartitionSpec as P

BLK_SHARD = 64
CAP = 4
META = 8
CHUNK = 8


def xor(a, b, n):
    out = jnp.int32(0)
    bit = 1
    while bit < n:
        x = lax.rem(lax.div(a, jnp.int32(bit)), jnp.int32(2))
        y = lax.rem(lax.div(b, jnp.int32(bit)), jnp.int32(2))
        out = out + bit * (x + y - 2 * x * y)
        bit *= 2
    return out


def kernel(
    nrep, nshard, limit,
    own_ref, loc_ref, cnt_ref, grads_ref, out_ref,
    masked, stg, recv, acc, tot, invt, part, norms,
    send_sem, recv_sem, nsend_sem, nrecv_sem,
):
    nblocks, rows, width = grads_ref.shape
    prow = rows // nrep
    peers = nrep * nshard
    rep = lax.axis_index("rep")
    shard = lax.axis_index("shard")

    def peer(k):
        ks, kr = lax.div(k, jnp.int32(nrep)), lax.rem(k, jnp.int32(nrep))
        return (xor(rep, kr, nrep), xor(shard, ks, nshard))

    barrier = pltpu.get_barrier_semaphore()

    def greet(i, carry):
        pl.semaphore_signal(
            barrier, inc=1, device_id=peer(i), device_id_type=pl.DeviceIdType.MESH
        )
        return carry

    lax.fori_loop(1, peers, greet, 0)

    cntf = cnt_ref[...].astype(jnp.float32)
    cols = cntf.T
    for b in range(nblocks):
        masked[b] = jnp.where(cols[:, b : b + 1] > 0, grads_ref[b], jnp.float32(0.0))

    def pack(i, carry):
        ks = nshard - 1 - i
        owner = xor(shard, ks, nshard)

        def scan(b, state):
            seen, src, ids = state
            hit = own_ref[b] == owner
            loc = loc_ref[b]
            take = [hit & (seen == c) for c in range(CAP)]
            src = tuple(jnp.where(take[c], b, src[c]) for c in range(CAP))
            ids = tuple(jnp.where(take[c], loc, ids[c]) for c in range(CAP))
            return (seen + hit.astype(jnp.int32), src, ids)

        zero, none = jnp.int32(0), jnp.int32(-1)
        unused, src, ids = lax.fori_loop(
            0, nblocks, scan, (zero, (zero,) * CAP, (none,) * CAP), unroll=16
        )
        for c in range(CAP):
            line = cnt_ref[pl.ds(src[c], 1), :].astype(jnp.float32)
            name = jnp.full((1, width), ids[c], jnp.int32).astype(jnp.float32)
            for kr in range(nrep):
                k = ks * nrep + kr
                first = pl.multiple_of(xor(rep, jnp.int32(kr), nrep) * prow, prow)
                stg[k, pl.ds(META + c * prow, prow), :] = masked[src[c], pl.ds(first, prow), :]
                stg[k, pl.ds(c, 1), :] = line
                stg[k, pl.ds(CAP + c, 1), :] = name
        return carry

    lax.fori_loop(0, nshard, pack, 0)
    acc[...] = jnp.zeros_like(acc)
    tot[...] = jnp.zeros_like(tot)

    pl.semaphore_wait(barrier, peers - 1)

    def message(k):
        return pltpu.make_async_remote_copy(
            src_ref=stg.at[k],
            dst_ref=recv.at[k],
            send_sem=send_sem.at[k],
            recv_sem=recv_sem.at[k],
            device_id=peer(k),
            device_id_type=pl.DeviceIdType.MESH,
        )

    def send(i, carry):
        message(peers - 1 - i).start()
        return carry

    lax.fori_loop(0, peers - 1, send, 0)

    def add(source, k):
        names = [source[k, pl.ds(CAP + c, 1), :] for c in range(CAP)]
        lines = [source[k, pl.ds(c, 1), :] for c in range(CAP)]
        block = lax.broadcasted_iota(jnp.int32, (BLK_SHARD, width), 0).astype(jnp.float32)
        total = tot[...]
        for c in range(CAP):
            total = total + jnp.where(block == names[c], lines[c], jnp.float32(0.0))
        tot[...] = total

        def some(j, carry):
            at = pl.multiple_of(j * CHUNK, CHUNK)
            value = [acc[at + t] for t in range(CHUNK)]
            for c in range(CAP):
                held = source[k, pl.ds(META + c * prow, prow), :]
                name = jnp.broadcast_to(names[c], (prow, width))
                for t in range(CHUNK):
                    hot = name == (at + t).astype(jnp.float32)
                    value[t] = value[t] + jnp.where(hot, held, jnp.float32(0.0))
            for t in range(CHUNK):
                acc[at + t] = value[t]
            return carry

        lax.fori_loop(0, BLK_SHARD // CHUNK, some, 0)

    add(stg, 0)

    def take(k):
        message(k).wait_recv()
        add(recv, k)

    def near(k, carry):
        take(k)
        return carry

    def far(i, carry):
        take(peers - 1 - i)
        return carry

    lax.fori_loop(1, peers // 2, near, 0)
    lax.fori_loop(0, peers - peers // 2, far, 0)

    def sent(k, carry):
        message(k).wait_send()
        return carry

    lax.fori_loop(1, peers, sent, 0)

    invt[...] = (jnp.float32(1.0) / jnp.maximum(tot[...], jnp.float32(1.0))).T
    inv = invt[pl.ds(pl.multiple_of(rep * prow, prow), prow), :]
    square = jnp.zeros((prow, width), jnp.float32)
    for t in range(BLK_SHARD):
        mean = acc[t] * inv[:, t : t + 1]
        acc[t] = mean
        square = square + mean * mean
    part[...] = jnp.sum(square.reshape(prow // 8, 8, width), axis=0)

    def norm(k):
        return pltpu.make_async_remote_copy(
            src_ref=part,
            dst_ref=norms.at[k],
            send_sem=nsend_sem.at[k],
            recv_sem=nrecv_sem.at[k],
            device_id=peer(k),
            device_id_type=pl.DeviceIdType.MESH,
        )

    def nsend(i, carry):
        norm(peers - 1 - i).start()
        return carry

    lax.fori_loop(0, peers - 1, nsend, 0)

    def ntake(k, total):
        norm(k).wait_recv()
        return total + norms[k]

    total = lax.fori_loop(1, peers, ntake, part[...])
    norm2 = jnp.sum(jnp.sum(total, axis=0, keepdims=True), axis=1, keepdims=True)
    scale = jnp.minimum(jnp.float32(1.0), limit / jnp.sqrt(norm2 + jnp.float32(1e-06)))
    for t in range(BLK_SHARD):
        out_ref[t] = acc[t] * scale

    def nsent(k, carry):
        norm(k).wait_send()
        return carry

    lax.fori_loop(1, peers, nsent, 0)


def local(nrep, nshard, grads, counts, block_owner, block_local):
    nblocks, rows, width = grads.shape[2:]
    peers = nrep * nshard
    prow = rows // nrep
    limit = math.sqrt(BLK_SHARD * nshard * rows * width) * 0.2
    body = functools.partial(kernel, nrep, nshard, limit)
    smem = pl.BlockSpec(memory_space=pltpu.SMEM)
    vmem = pl.BlockSpec(memory_space=pltpu.VMEM)
    size = META + CAP * prow
    return pl.pallas_call(
        body,
        out_shape=jax.ShapeDtypeStruct((BLK_SHARD, prow, width), jnp.float32),
        in_specs=[smem, smem, vmem, vmem],
        out_specs=vmem,
        scratch_shapes=[
            pltpu.VMEM((nblocks, rows, width), jnp.float32),
            pltpu.VMEM((peers, size, width), jnp.float32),
            pltpu.VMEM((peers, size, width), jnp.float32),
            pltpu.VMEM((BLK_SHARD, prow, width), jnp.float32),
            pltpu.VMEM((BLK_SHARD, width), jnp.float32),
            pltpu.VMEM((width, BLK_SHARD), jnp.float32),
            pltpu.VMEM((8, width), jnp.float32),
            pltpu.VMEM((peers, 8, width), jnp.float32),
            pltpu.SemaphoreType.DMA((peers,)),
            pltpu.SemaphoreType.DMA((peers,)),
            pltpu.SemaphoreType.DMA((peers,)),
            pltpu.SemaphoreType.DMA((peers,)),
        ],
        compiler_params=pltpu.CompilerParams(collective_id=0, has_side_effects=True),
        name="exchange",
    )(
        block_owner.reshape(nblocks),
        block_local.reshape(nblocks),
        counts.reshape(nblocks, rows),
        grads.reshape(nblocks, rows, width),
    )


def solution(mesh):
    body = functools.partial(local, mesh.shape["rep"], mesh.shape["shard"])
    return jax.shard_map(
        body,
        mesh=mesh,
        in_specs=(
            P("rep", "shard", None, None, None),
            P("rep", "shard", None, None),
            P("rep", "shard", None, None),
            P("rep", "shard", None),
        ),
        out_specs=P("shard", "rep", None),
        check_vma=False,
    )
```

time: 171 us -> 73.2 us (0.43); the launches traced: 169 us -> 73.1 us
  waiting for transfers between devices: 75.7 us -> 0 us
  Pallas kernels: 0 us -> 70.8 us
  blocking collectives: 45.1 us -> 0 us
  starting transfers between devices: 19.6 us -> 0 us
  local copies, waits for them, and re-layouts: 18.3 us -> 2.26 us
  other arithmetic: 7.37 us -> 0 us
  matrix products: 2.21 us -> 0 us
    all_to_all x5 -> x0, waiting for transfers between devices: 75.7 us -> none  [the longest x1 44.8 us: local(): lax.all_to_all(lax.all_to_all(send_vals, 'rep', split_axis=2, concat_axis...]
    pallas_call x0 -> x1, Pallas kernels: none -> 70.8 us  [local(): pl.pallas_call(body, out_shape=jax.ShapeDtypeStruct((BLK_SHARD, prow, wid...]
    psum x1 -> x0, blocking collectives: 37.2 us -> none  [local(): norm2 = lax.psum(jnp.sum(mean * mean), ('rep', 'shard'))]
    all_to_all x5 -> x0, starting transfers between devices: 19.6 us -> none  [the longest x1 5.83 us: local(): lax.all_to_all(lax.all_to_all(id_parts, 'rep', split_axis=2, concat_axis=...]
    all_to_all x1 -> x0, blocking collectives: 7.84 us -> none  [local(): lax.all_to_all(id_parts, 'rep', split_axis=2, concat_axis=1, tiled=True)]
    all_to_all x9 -> x0, local copies, waits for them, and re-layouts: 4.64 us -> none  [the longest x2 2.79 us: local(): lax.all_to_all(send_vals, 'rep', split_axis=2, concat_axis=1, tiled=True)]
    reshape x2 -> x0, local copies, waits for them, and re-layouts: 2.85 us -> none  [the longest x1 2.7 us: local(): send_vals = send_vals.reshape(nshard, CAP, rows, width)]
    unnamed x5 -> x1, local copies, waits for them, and re-layouts: 4.97 us -> 2.26 us
  transfers between devices with their start and end apart: 5 -> 0, of which waited for: 4 -> 0; matrix products, arithmetic and copies ran while one was open for 9% -> 0% of each run, Pallas kernels for 0% -> 0%
where the time goes in v1:
time: 73.2 us; the launch traced here: 73.1 us
  Pallas kernels  70.8 us (97%)
  local copies, waits for them, and re-layouts  2.26 us (3%)
    pallas_call x1, Pallas kernels, local(): pl.pallas_call(body, out_shape=jax.ShapeDtypeStruct((BLK_SHARD, prow, wid...  70.8 us
    unnamed x1, local copies, waits for them, and re-layouts  2.26 us

profile of v1, /device:TPU:0, one launch (start us, length us, event | category | flops | bytes accessed | tf_op | source)
XLA Modules:
  0.0 73.1 jit_solution(5944156862392522157)
XLA Ops:
  0.0 70.8 %exchange.1 = f32[64,32,128]{2,1,0:T(8,128)} custom-call(s32[16]{0:T(128)} %bitcast.6, s32[16]{0:T(128)} %bitcast.7, s32[16,128]{1,0:T(8,128)} %bitcast.5, f32[16,128,128]{2,1,0:T(8,128)} %bitcast.4), custom_call_target="tpu_custom_call" | custom-call | tf_op jit(solution)/shard_map/exchange/pallas_call | solution.py:207
  70.8 2.3 %copy.6 = f32[64,32,128]{2,1,0:T(8,128)} copy(f32[64,32,128]{2,1,0:T(8,128)} %exchange.1) | data formatting | bytes 2097152

commit v2 on v1

--- a/solution.py
+++ b/solution.py
@@ -10,7 +10,7 @@
 
 BLK_SHARD = 64
 CAP = 4
-META = 8
+META = 2
 CHUNK = 8
 
 
@@ -27,13 +27,14 @@
 
 def kernel(
     nrep, nshard, limit,
-    own_ref, loc_ref, cnt_ref, grads_ref, out_ref,
-    masked, stg, recv, acc, tot, invt, part, norms,
-    send_sem, recv_sem, nsend_sem, nrecv_sem,
+    own_ref, loc_ref, cnt_ref, grads_ref, out_ref, scale_ref,
+    masked, stg, recv, acc, tot, part, norms,
+    out_sem, send_sem, recv_sem, nsend_sem, nrecv_sem,
 ):
     nblocks, rows, width = grads_ref.shape
     prow = rows // nrep
     peers = nrep * nshard
+    size = CAP * prow + META
     rep = lax.axis_index("rep")
     shard = lax.axis_index("shard")
 
@@ -56,8 +57,12 @@
     for b in range(nblocks):
         masked[b] = jnp.where(cols[:, b : b + 1] > 0, grads_ref[b], jnp.float32(0.0))
 
-    def pack(i, carry):
-        ks = nshard - 1 - i
+    def order(i):
+        far, near = lax.div(i, jnp.int32(2)), lax.rem(i, jnp.int32(2))
+        return nshard - 1 - far - near * (nshard // 2)
+
+    def pack(i):
+        ks = order(i)
         owner = xor(shard, ks, nshard)
 
         def scan(b, state):
@@ -73,53 +78,61 @@
         unused, src, ids = lax.fori_loop(
             0, nblocks, scan, (zero, (zero,) * CAP, (none,) * CAP), unroll=16
         )
+        lane = lax.broadcasted_iota(jnp.int32, (1, width), 1)
+        name = jnp.full((1, width), -1, jnp.int32)
         for c in range(CAP):
-            line = cnt_ref[pl.ds(src[c], 1), :].astype(jnp.float32)
-            name = jnp.full((1, width), ids[c], jnp.int32).astype(jnp.float32)
-            for kr in range(nrep):
-                k = ks * nrep + kr
-                first = pl.multiple_of(xor(rep, jnp.int32(kr), nrep) * prow, prow)
-                stg[k, pl.ds(META + c * prow, prow), :] = masked[src[c], pl.ds(first, prow), :]
-                stg[k, pl.ds(c, 1), :] = line
-                stg[k, pl.ds(CAP + c, 1), :] = name
-        return carry
-
-    lax.fori_loop(0, nshard, pack, 0)
-    acc[...] = jnp.zeros_like(acc)
-    tot[...] = jnp.zeros_like(tot)
-
-    pl.semaphore_wait(barrier, peers - 1)
+            name = jnp.where((lane >= c * prow) & (lane < (c + 1) * prow), ids[c], name)
+        name = name.astype(jnp.float32)
+        lines = [cnt_ref[pl.ds(src[c], 1), :].astype(jnp.float32) for c in range(CAP)]
+        for p in range(nrep):
+            k = ks * nrep + xor(rep, jnp.int32(p), nrep)
+            line = jnp.zeros((1, width), jnp.float32)
+            for c in range(CAP):
+                stg[k, pl.ds(c * prow, prow), :] = masked[src[c], pl.ds(p * prow, prow), :]
+                turned = pltpu.roll(lines[c], (c - p) * prow % width, 1)
+                line = jnp.where((lane >= c * prow) & (lane < (c + 1) * prow), turned, line)
+            stg[k, pl.ds(CAP * prow, 1), :] = line
+            stg[k, pl.ds(CAP * prow + 1, 1), :] = name
 
     def message(k):
         return pltpu.make_async_remote_copy(
-            src_ref=stg.at[k],
-            dst_ref=recv.at[k],
+            src_ref=stg.at[k, pl.ds(0, size)],
+            dst_ref=recv.at[k, pl.ds(0, size)],
             send_sem=send_sem.at[k],
             recv_sem=recv_sem.at[k],
             device_id=peer(k),
             device_id_type=pl.DeviceIdType.MESH,
         )
 
-    def send(i, carry):
-        message(peers - 1 - i).start()
-        return carry
-
-    lax.fori_loop(0, peers - 1, send, 0)
+    def send(i, first):
+        for kr in range(nrep - 1, first - 1, -1):
+            message(order(i) * nrep + kr).start()
+
+    pack(jnp.int32(0))
+    pl.semaphore_wait(barrier, peers - 1)
+
+    def step(i, carry):
+        pack(i)
+        send(i - 1, 0)
+        return carry
+
+    lax.fori_loop(1, nshard, step, 0)
+    send(jnp.int32(nshard - 1), 1)
+    acc[...] = jnp.zeros_like(acc)
+    tot[...] = jnp.zeros_like(tot)
 
     def add(source, k):
-        names = [source[k, pl.ds(CAP + c, 1), :] for c in range(CAP)]
-        lines = [source[k, pl.ds(c, 1), :] for c in range(CAP)]
+        line = source[k, pl.ds(CAP * prow, 1), :]
+        name = source[k, pl.ds(CAP * prow + 1, 1), :]
+        names = [jnp.broadcast_to(name[:, c * prow : c * prow + 1], (1, width)) for c in range(CAP)]
         block = lax.broadcasted_iota(jnp.int32, (BLK_SHARD, width), 0).astype(jnp.float32)
-        total = tot[...]
-        for c in range(CAP):
-            total = total + jnp.where(block == names[c], lines[c], jnp.float32(0.0))
-        tot[...] = total
+        tot[...] = tot[...] + jnp.where(block == name, line, jnp.float32(0.0))
 
         def some(j, carry):
             at = pl.multiple_of(j * CHUNK, CHUNK)
             value = [acc[at + t] for t in range(CHUNK)]
             for c in range(CAP):
-                held = source[k, pl.ds(META + c * prow, prow), :]
+                held = source[k, pl.ds(c * prow, prow), :]
                 name = jnp.broadcast_to(names[c], (prow, width))
                 for t in range(CHUNK):
                     hot = name == (at + t).astype(jnp.float32)
@@ -136,16 +149,18 @@
         message(k).wait_recv()
         add(recv, k)
 
-    def near(k, carry):
-        take(k)
-        return carry
-
-    def far(i, carry):
-        take(peers - 1 - i)
-        return carry
-
-    lax.fori_loop(1, peers // 2, near, 0)
-    lax.fori_loop(0, peers - peers // 2, far, 0)
+    def group(h, carry):
+        for near in (1, 0):
+            ks = order(2 * h + near)
+            for kr in range(nrep - 1, -1, -1):
+                k = ks * nrep + kr
+                if near and kr == 0:
+                    pl.when(k > 0)(functools.partial(take, k))
+                else:
+                    take(k)
+        return carry
+
+    lax.fori_loop(0, nshard // 2, group, 0)
 
     def sent(k, carry):
         message(k).wait_send()
@@ -153,13 +168,17 @@
 
     lax.fori_loop(1, peers, sent, 0)
 
-    invt[...] = (jnp.float32(1.0) / jnp.maximum(tot[...], jnp.float32(1.0))).T
-    inv = invt[pl.ds(pl.multiple_of(rep * prow, prow), prow), :]
+    total = tot[...]
+    for c in range(1, CAP):
+        total = total + pltpu.roll(tot[...], -c * prow % width, 1)
+    inv = (jnp.float32(1.0) / jnp.maximum(total, jnp.float32(1.0))).T[:prow, :]
     square = jnp.zeros((prow, width), jnp.float32)
     for t in range(BLK_SHARD):
         mean = acc[t] * inv[:, t : t + 1]
         acc[t] = mean
         square = square + mean * mean
+    mean_copy = pltpu.make_async_copy(acc, out_ref, out_sem)
+    mean_copy.start()
     part[...] = jnp.sum(square.reshape(prow // 8, 8, width), axis=0)
 
     def norm(k):
@@ -185,8 +204,8 @@
     total = lax.fori_loop(1, peers, ntake, part[...])
     norm2 = jnp.sum(jnp.sum(total, axis=0, keepdims=True), axis=1, keepdims=True)
     scale = jnp.minimum(jnp.float32(1.0), limit / jnp.sqrt(norm2 + jnp.float32(1e-06)))
-    for t in range(BLK_SHARD):
-        out_ref[t] = acc[t] * scale
+    scale_ref[...] = scale
+    mean_copy.wait()
 
     def nsent(k, carry):
         norm(k).wait_send()
@@ -203,21 +222,24 @@
     body = functools.partial(kernel, nrep, nshard, limit)
     smem = pl.BlockSpec(memory_space=pltpu.SMEM)
     vmem = pl.BlockSpec(memory_space=pltpu.VMEM)
-    size = META + CAP * prow
-    return pl.pallas_call(
+    size = -(-(META + CAP * prow) // 8) * 8
+    mean, scale = pl.pallas_call(
         body,
-        out_shape=jax.ShapeDtypeStruct((BLK_SHARD, prow, width), jnp.float32),
+        out_shape=(
+            jax.ShapeDtypeStruct((BLK_SHARD, prow, width), jnp.float32),
+            jax.ShapeDtypeStruct((1, 1), jnp.float32),
+        ),
         in_specs=[smem, smem, vmem, vmem],
-        out_specs=vmem,
+        out_specs=(pl.BlockSpec(memory_space=pl.ANY), vmem),
         scratch_shapes=[
             pltpu.VMEM((nblocks, rows, width), jnp.float32),
             pltpu.VMEM((peers, size, width), jnp.float32),
             pltpu.VMEM((peers, size, width), jnp.float32),
             pltpu.VMEM((BLK_SHARD, prow, width), jnp.float32),
             pltpu.VMEM((BLK_SHARD, width), jnp.float32),
-            pltpu.VMEM((width, BLK_SHARD), jnp.float32),
             pltpu.VMEM((8, width), jnp.float32),
             pltpu.VMEM((peers, 8, width), jnp.float32),
+            pltpu.SemaphoreType.DMA,
             pltpu.SemaphoreType.DMA((peers,)),
             pltpu.SemaphoreType.DMA((peers,)),
             pltpu.SemaphoreType.DMA((peers,)),
@@ -231,6 +253,7 @@
         counts.reshape(nblocks, rows),
         grads.reshape(nblocks, rows, width),
     )
+    return mean * scale.reshape(())
 
 
 def solution(mesh):

time: 73.2 us -> 74.5 us (1.018)
  other arithmetic: 0 us -> 2.84 us
  local copies, waits for them, and re-layouts: 2.26 us -> 0 us
    mul x0 -> x1, other arithmetic: none -> 2.84 us  [local(): return mean * scale.reshape(())]
    unnamed x1 -> x0, local copies, waits for them, and re-layouts: 2.26 us -> none
where the time goes in v2:
time: 74.5 us; the launch traced here: 74.3 us
  Pallas kernels  71.5 us (96%)
  other arithmetic  2.84 us (4%)
    pallas_call x1, Pallas kernels, local(): pl.pallas_call(body, out_shape=(jax.ShapeDtypeStruct((BLK_SHARD, prow, wi...  71.5 us
    mul x1, other arithmetic, local(): return mean * scale.reshape(())  2.84 us

profile of v2, /device:TPU:0, one launch (start us, length us, event | category | flops | bytes accessed | tf_op | source)
XLA Modules:
  0.0 74.3 jit_solution(4735164105426711123)
XLA Ops:
  0.0 71.5 %exchange.1 = (f32[64,32,128]{2,1,0:T(8,128)}, f32[1,1]{1,0:T(1,128)}) custom-call(s32[16]{0:T(128)} %bitcast.7, s32[16]{0:T(128)} %bitcast.8, s32[16,128]{1,0:T(8,128)} %bitcast.6, f32[16,128,128]{2,1,0:T(8,128)} %bitcast.5), custom_call_target="tpu_custom_call" | custom-call | tf_op jit(solution)/shard_map/exchange/pallas_call | solution.py:226
  71.5 2.8 %broadcast_multiply_fusion = f32[64,32,128]{2,1,0:T(8,128)} fusion(f32[64,32,128]{2,1,0:T(8,128)} %get-tuple-element.7, f32[]{:T(128)} %bitcast.4), kind=kLoop, calls=%fused_computation | loop fusion | flops 262144 | bytes 2097156 | tf_op jit(solution)/shard_map/mul | solution.py:256

commit v3 on v1

--- a/solution.py
+++ b/solution.py
@@ -101,7 +101,8 @@
         )
 
     def send(i, carry):
-        message(peers - 1 - i).start()
+        far, near = lax.div(i, jnp.int32(2)), lax.rem(i, jnp.int32(2))
+        message(peers - 1 - far - near * (peers // 2)).start()
         return carry
 
     lax.fori_loop(0, peers - 1, send, 0)

time: 73.2 us -> 70.6 us (0.964)
  Pallas kernels: 70.8 us -> 68.2 us
    pallas_call x1, Pallas kernels: 70.8 us -> 68.2 us  [local(): pl.pallas_call(body, out_shape=jax.ShapeDtypeStruct((BLK_SHARD, prow, wid...]
where the time goes in v3:
time: 70.6 us; the launch traced here: 70.4 us
  Pallas kernels  68.2 us (97%)
  local copies, waits for them, and re-layouts  2.26 us (3%)
    pallas_call x1, Pallas kernels, local(): pl.pallas_call(body, out_shape=jax.ShapeDtypeStruct((BLK_SHARD, prow, wid...  68.2 us
    unnamed x1, local copies, waits for them, and re-layouts  2.26 us

profile of v3, /device:TPU:0, one launch (start us, length us, event | category | flops | bytes accessed | tf_op | source)
XLA Modules:
  0.0 70.4 jit_solution(16674203463713759306)
XLA Ops:
  0.0 68.2 %exchange.1 = f32[64,32,128]{2,1,0:T(8,128)} custom-call(s32[16]{0:T(128)} %bitcast.6, s32[16]{0:T(128)} %bitcast.7, s32[16,128]{1,0:T(8,128)} %bitcast.5, f32[16,128,128]{2,1,0:T(8,128)} %bitcast.4), custom_call_target="tpu_custom_call" | custom-call | tf_op jit(solution)/shard_map/exchange/pallas_call | solution.py:208
  68.2 2.3 %copy.6 = f32[64,32,128]{2,1,0:T(8,128)} copy(f32[64,32,128]{2,1,0:T(8,128)} %exchange.1) | data formatting | bytes 2097152
